TPU v7x, 256 devices: a 2x2x32 block of a 4x8x32 slice. The times are simulated.
256 devices in a mesh: parts: 4 (over y, x), dp: 64 (over z, core).
Axes of the slice: x: 2, y: 2, z: 32, core: 2. Of those that a mesh axis runs over, the one named last changes fastest.
The devices are a block of a 4x8x32 slice.
Arguments:
- activations: bfloat16 [65536, 14336], P(('parts', 'dp')), parts along dimension 0, may hold values from -6 to 6
- out_grads: bfloat16 [65536, 4096], P(('parts', 'dp')), parts along dimension 0, may hold values from -6 to 6
- lengths: int32 [256, 4], P(('parts', 'dp')), parts along dimension 0, may hold values from 1 to 128, 256 in all within a row
- proj_in: bfloat16 [14336, 64], replicated, may hold values from -0.046875 to 0.046875
- proj_out: bfloat16 [4096, 64], replicated, may hold values from -0.09375 to 0.09375
- queries: bfloat16 [8192, 4096], P(('parts', 'dp')), parts along dimension 0, may hold values from -0.01171875 to 0.01171875
Outputs:
- scores: bfloat16 [1024, 2048], P(('parts', 'dp')), parts along dimension 0
There are 4 independent parts, one for each index of `parts`. A program takes and returns all parts, laid end to end along the dimension named above; an argument that names none is the same for every part. Nothing has to cross between parts.
Inputs may be any that keep to these rules, and one draw needn't show every extreme that they name: Each row of lengths sums to 256, and one entry of each row equals 128.
All inputs are finite; a program needn't handle non-finite values.
Results may differ from a plain program's by a relative error of at most 0.0065.
Values may be sent and summed in bfloat16 or wider, within the bound.
A program may use at most 128 MiB of HBM per device.

v0:
```python
import jax
import jax.numpy as jnp
from jax import lax
from jax.sharding import PartitionSpec as P


def local(activations, out_grads, lengths, proj_in, proj_out, queries):
    tok_count = activations.shape[0]
    rank_size = proj_in.shape[1]
    proj_acts = jnp.dot(activations, proj_in, preferred_element_type=jnp.float32).astype(
        jnp.bfloat16
    )
    proj_grads = jnp.dot(out_grads, proj_out, preferred_element_type=jnp.float32).astype(
        jnp.bfloat16
    )
    counts = lengths[0]
    tok_ends = jnp.cumsum(counts)
    tok_starts = tok_ends - counts
    position = jnp.arange(tok_count, dtype=jnp.int32)
    member = (
        (position[None, :] >= tok_starts[:, None]) & (position[None, :] < tok_ends[:, None])
    ).astype(jnp.bfloat16)
    masked_grads = member[:, :, None] * proj_grads[None, :, :]
    summed = jnp.einsum("eti,tj->eij", masked_grads, proj_acts, preferred_element_type=jnp.float32)
    example_grads = summed.reshape(counts.shape[0], rank_size * rank_size).astype(jnp.bfloat16)
    contract = (((1,), (1,)), ((), ()))
    scores = lax.dot_general(
        example_grads,
        lax.all_gather(queries, "dp", axis=0, tiled=True),
        contract,
        preferred_element_type=jnp.float32,
    )
    return scores.astype(jnp.bfloat16)


def solution(mesh):
    in_specs = (
        P(("parts", "dp"), None),
        P(("parts", "dp"), None),
        P(("parts", "dp"), None),
        P(),
        P(),
        P(("parts", "dp"), None),
    )
    out_specs = P(("parts", "dp"), None)
    return jax.shard_map(local, mesh=mesh, in_specs=in_specs, out_specs=out_specs, check_vma=False)
```

profile of v0, /device:TPU:37, one launch (start us, length us, event | category | flops | bytes accessed | tf_op | source)
XLA Modules:
  0.0 188.2 jit_solution(3009798860218271106)
XLA Ops:
  6.5 0.0 copy-start
  6.6 0.0 all-gather.2.cloned.1.call-start
  6.6 0.7 all-gather.2.cloned.1.call-update
  7.3 0.8 reduce-window.7
  8.1 0.7 bitcast_subtract_fusion
  8.8 0.1 fusion.5
  8.9 0.0 copy-done
  8.9 1.8 convolution_convert_fusion.3
  10.7 6.2 %convolution_convert_fusion.1 = bf16[4,64,64]{2,1,0:T(8,128)(2,1)S(1)} fusion(bf16[256,14336]{1,0:T(8,128)(2,1)} %param.6, bf16[14336,64]{0,1:T(8,128)(2,1)} %param.9, bf16[256,64]{0,1:T(8,128)(2,1)S(1)} %convolution_convert_fusion.3, bf16[4,256]{1,0:T(4,128)(2,1)S(1)} %fusion.5), kind=kOutput, calls=%fused_computation.1 | convolution fusion | flops 478248960 | bytes 9242624 | tf_op jit(solution)/shard_map/eti,tj->eij/dot_general | solution.py:24
  16.9 0.1 convert_element_type.26
  17.0 153.5 %all-gather.2.cloned.1.call-done = bf16[2048,4096]{1,0:T(8,128)(2,1)} async-done(((bf16[32,4096]{1,0:T(8,128)(2,1)}), bf16[2048,4096]{1,0:T(8,128)(2,1)}) %all-gather.2.cloned.1.call-update) | async-done | bytes 16777232 | tf_op jit(solution)/shard_map/all_gather | solution.py:29
  170.5 10.8 %convolution_convert_fusion = bf16[4,2048]{1,0:T(4,128)(2,1)} fusion(bf16[4,4096]{1,0:T(4,128)(2,1)S(1)} %convert_element_type.26, bf16[2048,4096]{1,0:T(8,128)(2,1)} %all-gather.2.cloned.1.call-done), kind=kOutput, calls=%fused_computation | convolution fusion | flops 67117056 | bytes 16826368 | tf_op jit(solution)/shard_map/dot_general | solution.py:27
Async XLA Ops:
  6.5 2.3 %copy-start = (bf16[256,4096]{1,0:T(8,128)(2,1)S(1)}, bf16[256,4096]{1,0:T(8,128)(2,1)}, u32[]{:S(2)}) copy-start(bf16[256,4096]{1,0:T(8,128)(2,1)} %param.7) | copy-start | bytes 6291460
  6.6 163.9 %all-gather.2.cloned.1.call-start = ((), (), s32[]{:S(2)}) async-start(), calls=%async_computation | async-start | bytes 17039360 | tf_op jit(solution)/shard_map/all_gather | solution.py:29
Sparse Core Ops, SparseCore 0:
  9.2 161.2 all-gather.1
where the time goes:
time: 188 us
  waiting for transfers between devices  154 us (82%)
  matrix products  18.8 us (10%)
  between operations  13.4 us (7%)
    all_gather x1, waiting for transfers between devices, local(): lax.all_gather(queries, 'dp', axis=0, tiled=True)  153 us
    dot_general x1, matrix products, local(): lax.dot_general(example_grads, lax.all_gather(queries, 'dp', axis=0, tile...  10.8 us
    dot_general x1, matrix products, local(): jnp.einsum('eti,tj->eij', masked_grads, proj_acts, preferred_element_type...  6.21 us
  transfers between devices with their start and end apart: 1, of which 1 were waited for; matrix products, arithmetic and copies ran while one was open for 5% of the time, Pallas kernels for 0%

commit v1 on v0

--- a/solution.py
+++ b/solution.py
@@ -2,6 +2,12 @@
 import jax.numpy as jnp
 from jax import lax
 from jax.sharding import PartitionSpec as P
+
+
+def tiled_gather(x, axis, dim):
+    length = lax.axis_size(axis)
+    repeats = [length if d == dim else 1 for d in range(x.ndim)]
+    return lax.all_to_all(jnp.tile(x, repeats), axis, split_axis=dim, concat_axis=dim, tiled=True)
 
 
 def local(activations, out_grads, lengths, proj_in, proj_out, queries):
@@ -25,10 +31,7 @@
     example_grads = summed.reshape(counts.shape[0], rank_size * rank_size).astype(jnp.bfloat16)
     contract = (((1,), (1,)), ((), ()))
     scores = lax.dot_general(
-        example_grads,
-        lax.all_gather(queries, "dp", axis=0, tiled=True),
-        contract,
-        preferred_element_type=jnp.float32,
+        example_grads, tiled_gather(queries, "dp", 0), contract, preferred_element_type=jnp.float32
     )
     return scores.astype(jnp.bfloat16)
 

time: 188 us -> 1510 us (8.03); the launches traced: 188 us -> 1490 us
  waiting for transfers between devices: 154 us -> 1430 us
  starting transfers between devices: 0.01 us -> 34.5 us
    all_to_all x0 -> x1, waiting for transfers between devices: none -> 1430 us  [tiled_gather(): lax.all_to_all(jnp.tile(x, repeats), axis, split_axis=dim, concat_axis=di...]
    all_gather x1 -> x0, waiting for transfers between devices: 153 us -> none  [local(): lax.all_gather(queries, 'dp', axis=0, tiled=True)]
    all_to_all x0 -> x1, starting transfers between devices: none -> 34.5 us  [tiled_gather(): lax.all_to_all(jnp.tile(x, repeats), axis, split_axis=dim, concat_axis=di...]
  transfers between devices with their start and end apart: 1 -> 1, of which waited for: 1 -> 1; matrix products, arithmetic and copies ran while one was open for 5% -> 0% of each run, Pallas kernels for 0% -> 0%
where the time goes in v1:
time: 1510 us; the launch traced here: 1490 us
  waiting for transfers between devices  1430 us (95%)
  starting transfers between devices  34.5 us (2%)
  matrix products  17.7 us (1%)
    all_to_all x1, waiting for transfers between devices, tiled_gather(): lax.all_to_all(jnp.tile(x, repeats), axis, split_axis=dim, concat_axis=di...  1430 us
    all_to_all x1, starting transfers between devices, tiled_gather(): lax.all_to_all(jnp.tile(x, repeats), axis, split_axis=dim, concat_axis=di...  34.5 us
  transfers between devices with their start and end apart: 1, of which 1 were waited for; matrix products, arithmetic and copies ran while one was open for 0% of the time, Pallas kernels for 0%

profile of v1, /device:TPU:37, one launch (start us, length us, event | category | flops | bytes accessed | tf_op | source)
XLA Modules:
  0.0 1486.6 jit_solution(3080879991786979918)
XLA Ops:
  0.0 0.0 copy-start
  0.0 6.9 tile.2
  6.9 0.0 copy-start.2
  6.9 0.0 copy-start.1
  6.9 34.5 %all-to-all-start = ((bf16[64,32,4096]{2,1,0:T(8,128)(2,1)}), bf16[64,32,4096]{2,1,0:T(8,128)(2,1)}, u32[]{:S(2)}, u32[]{:S(2)}) async-start(bf16[64,32,4096]{2,1,0:T(8,128)(2,1)} %tile.2), calls=%async_computation | async-start | bytes 33554432 | tf_op jit(solution)/shard_map/all_to_all | solution.py:10
  41.4 0.0 copy-done.2
  41.4 0.2 reduce-window.7
  41.6 0.1 fusion.5
  41.7 0.0 copy-done
  41.7 0.0 copy-done.1
  41.7 0.8 convolution_convert_fusion.3
  42.5 6.2 convolution_convert_fusion.1
  48.7 0.1 convert_element_type.26
  48.8 1427.0 %all-to-all-done = bf16[64,32,4096]{2,1,0:T(8,128)(2,1)} async-done(((bf16[64,32,4096]{2,1,0:T(8,128)(2,1)}), bf16[64,32,4096]{2,1,0:T(8,128)(2,1)}, u32[]{:S(2)}, u32[]{:S(2)}) %all-to-all-start) | async-done | bytes 16777248 | tf_op jit(solution)/shard_map/all_to_all | solution.py:10
  1475.8 10.8 convolution_convert_fusion
  (1 shorter events, 0.0 us)
Async XLA Ops:
  0.0 41.7 %copy-start = (bf16[256,4096]{1,0:T(8,128)(2,1)S(1)}, bf16[256,4096]{1,0:T(8,128)(2,1)}, u32[]{:S(2)}) copy-start(bf16[256,4096]{1,0:T(8,128)(2,1)} %param.7) | copy-start | bytes 6291460
  6.9 34.5 %copy-start.2 = (s32[1,4]{1,0:T(1,128)S(1)}, s32[1,4]{1,0:T(1,128)}, u32[]{:S(2)}) copy-start(s32[1,4]{1,0:T(1,128)} %param.8) | copy-start | bytes 52
  6.9 34.8 %copy-start.1 = (bf16[4096,64]{0,1:T(8,128)(2,1)S(1)}, bf16[4096,64]{0,1:T(8,128)(2,1)}, u32[]{:S(2)}) copy-start(bf16[4096,64]{0,1:T(8,128)(2,1)} %param.10) | copy-start | bytes 1572868
  6.9 1468.9 %all-to-all-start = ((bf16[64,32,4096]{2,1,0:T(8,128)(2,1)}), bf16[64,32,4096]{2,1,0:T(8,128)(2,1)}, u32[]{:S(2)}, u32[]{:S(2)}) async-start(bf16[64,32,4096]{2,1,0:T(8,128)(2,1)} %tile.2), calls=%async_computation | async-start | bytes 33554432 | tf_op jit(solution)/shard_map/all_to_all | solution.py:10
